TPU v7x, 32 devices: a whole 2x2x4 slice. The times are simulated.
32 devices in a mesh: freq: 16 (over z, x, core), grid: 2 (over y).
Axes of the slice: x: 2, y: 2, z: 4, core: 2. Of those that a mesh axis runs over, the one named last changes fastest.
Arguments:
- cross_spectra: float32 [2, 32, 256, 256], P(None, None, 'freq', 'grid'), as said below
- sensor_modes: float32 [32, 96, 256], P('freq', None, 'grid'), may hold values from -0.375 to 0.375
- source_modes: float32 [32, 96, 256], P('freq', None, 'grid'), may hold values from -6 to 6
- wavenumber: float32 [32, 96], P('freq'), may hold values from 0.5 to 2
- attenuation: float32 [32, 96], P('freq'), may hold values from 0.002 to 0.03
- mode_counts: int32 [32], P('freq'), may hold values from 48 to 96
Outputs:
- bartlett_power: float32 [64, 256], P('freq', 'grid')
Inputs may be any that keep to these rules, and one draw needn't show every extreme that they name: `cross_spectra`: each bin's matrix K_f is Hermitian and positive definite. Modes with index mode_counts[f] or more are left out in bin f.
All inputs are finite; a program needn't handle non-finite values.
Results may differ from a plain program's by a relative error of at most 0.0003.
Values sent between devices are 32-bit elements; how exact they have to be, the bound alone decides.
A program may use at most 128 MiB of HBM per device.

v0:
```python
import jax
import jax.numpy as jnp
from jax import lax
from jax.sharding import PartitionSpec as P

RANGES = 64
HIGH = lax.Precision.HIGHEST


def replica_terms(wave_row, atten_row, count, source_row, ranges):
    phase = wave_row[:, None] * ranges[None, :]
    magnitude = jnp.exp(-atten_row[:, None] * ranges[None, :]) / jnp.sqrt(phase)
    keep = (jnp.arange(source_row.shape[0], dtype=jnp.int32) < count).astype(jnp.float32)
    hankel_real = magnitude * jnp.cos(phase) * keep[:, None]
    hankel_imag = magnitude * jnp.sin(phase) * keep[:, None]
    coef_real = hankel_real[:, :, None] * source_row[:, None, :]
    coef_imag = hankel_imag[:, :, None] * source_row[:, None, :]
    return (coef_real, coef_imag)


def per_device(cross_spectra, sensor_modes, source_modes, wavenumber, attenuation, mode_counts):
    modes = sensor_modes.shape[1]
    bins_here = sensor_modes.shape[0]
    depth_here = source_modes.shape[2]
    total_bins = bins_here * lax.axis_size("freq")
    whole_spectra = lax.all_to_all(
        lax.all_to_all(cross_spectra, "freq", split_axis=1, concat_axis=2, tiled=True),
        "grid",
        split_axis=1,
        concat_axis=3,
        tiled=True,
    )
    whole_modes = lax.all_to_all(sensor_modes, "grid", split_axis=0, concat_axis=2, tiled=True)
    product = jnp.einsum("cbij,bmj->cbim", whole_spectra, whole_modes, precision=HIGH)
    projected = jnp.einsum("bmi,cbin->cbmn", whole_modes, product, precision=HIGH)
    gram = jnp.einsum("bmi,bni->bmn", whole_modes, whole_modes, precision=HIGH)
    stacked_local = jnp.concatenate([projected, gram[None]], 0)
    spectra = lax.all_gather(stacked_local, "grid", axis=1, tiled=True)
    count = RANGES // lax.axis_size("freq") * lax.axis_size("freq")
    ranges = 1.0 + jnp.arange(count, dtype=jnp.int32).astype(jnp.float32)

    def one_bin(bin_index, total):
        block = spectra[:, bin_index]
        coupling = jnp.concatenate(
            [jnp.concatenate([block[0], -block[1]], 1), jnp.concatenate([block[1], block[0]], 1)], 0
        )
        coef_real, coef_imag = replica_terms(
            wavenumber[bin_index],
            attenuation[bin_index],
            mode_counts[bin_index],
            source_modes[bin_index],
            ranges,
        )
        coefs = jnp.concatenate([coef_real, coef_imag], 0).reshape(2 * modes, count * depth_here)
        image = jnp.dot(coupling, coefs, precision=HIGH)
        weighted = jnp.einsum(
            "mn,cnx->cmx", block[2], coefs.reshape(2, modes, count * depth_here), precision=HIGH
        )
        weighted = weighted.reshape(2 * modes, count * depth_here)
        numer = jnp.sum(coefs * image, axis=0)
        denom = jnp.sum(coefs * weighted, axis=0)
        return total + (numer / denom).reshape(count, depth_here)

    summed = lax.fori_loop(0, bins_here, one_bin, jnp.zeros((count, depth_here), jnp.float32))
    return lax.psum_scatter(summed / total_bins, "freq", scatter_dimension=0, tiled=True)


def solution(mesh):
    placed = (
        P(None, None, "freq", "grid"),
        P("freq", None, "grid"),
        P("freq", None, "grid"),
        P("freq", None),
        P("freq", None),
        P("freq"),
    )
    return jax.shard_map(
        per_device, mesh=mesh, in_specs=placed, out_specs=P("freq", "grid"), check_vma=False
    )
```

profile of v0, /device:TPU:0, one launch (start us, length us, event | category | flops | bytes accessed | tf_op | source)
XLA Modules:
  0.0 178.7 jit_solution(12962401052543887064)
XLA Ops:
  0.0 1.1 copy.23
  1.2 21.5 %all_to_all.48 = f32[2,32,16,128]{3,2,0,1:T(8,128)S(1)} all-to-all(f32[2,32,16,128]{3,2,0,1:T(8,128)S(1)} %copy.23), channel_id=1, replica_groups=mesh['freq'=16,'grid'=2] {'freq'}, dimensions={1} | all-to-all | bytes 1048576 | tf_op jit(solution)/shard_map/all_to_all | solution.py:27
  22.6 3.3 %all-to-all-start = ((f32[2,96,128]{2,1,0:T(8,128)}), f32[2,96,128]{2,1,0:T(8,128)S(1)}, u32[]{:S(2)}, u32[]{:S(2)}) async-start(f32[2,96,128]{2,1,0:T(8,128)} %param.9), calls=%async_computation | async-start | bytes 196608 | tf_op jit(solution)/shard_map/all_to_all | solution.py:33
  26.0 0.8 copy.24
  26.8 3.4 %all-to-all-done = f32[2,96,128]{2,1,0:T(8,128)S(1)} async-done(((f32[2,96,128]{2,1,0:T(8,128)}), f32[2,96,128]{2,1,0:T(8,128)S(1)}, u32[]{:S(2)}, u32[]{:S(2)}) %all-to-all-start) | async-done | bytes 98336 | tf_op jit(solution)/shard_map/all_to_all | solution.py:33
  30.3 3.5 %all-to-all-start.2 = ((f32[2,2,256,128]{3,2,0,1:T(8,128)}), f32[2,2,256,128]{3,2,0,1:T(8,128)S(1)}, u32[]{:S(2)}, u32[]{:S(2)}) async-start(f32[2,2,256,128]{3,2,0,1:T(8,128)} %bitcast.6), calls=%async_computation.2 | async-start | bytes 1048576 | tf_op jit(solution)/shard_map/all_to_all | solution.py:26
  33.8 1.3 dynamic-slice
  35.8 0.1 copy.26
  35.8 0.1 reshape.252
  35.9 0.2 convolution_bitcast_fusion.3
  36.2 5.0 %all-to-all-done.2 = f32[2,2,256,128]{3,2,0,1:T(8,128)S(1)} async-done(((f32[2,2,256,128]{3,2,0,1:T(8,128)}), f32[2,2,256,128]{3,2,0,1:T(8,128)S(1)}, u32[]{:S(2)}, u32[]{:S(2)}) %all-to-all-start.2) | async-done | bytes 524320 | tf_op jit(solution)/shard_map/all_to_all | solution.py:26
  41.1 0.6 convolution_bitcast_fusion.1
  41.8 0.3 convolution_bitcast_fusion.2
  42.1 0.1 copy.28
  42.2 5.8 %all_gather.3 = f32[3,2,96,96]{3,2,0,1:T(8,128)S(1)} all-gather(f32[3,1,96,96]{3,2,0,1:T(8,128)S(1)} %copy.28), channel_id=1, replica_groups=mesh['freq'=16,'grid'=2] {'grid'}, dimensions={1}, use_global_device_ids=true | all-gather | bytes 331776 | tf_op jit(solution)/shard_map/all_gather | solution.py:38
  48.0 0.0 copy-done.2
  48.0 0.0 copy-done.3
  48.0 0.0 copy-done.4
  48.1 0.0 copy-done.1
  48.1 72.4 %while.15 = (s32[]{:T(128)}, f32[64,128]{1,0:T(8,128)S(1)}, f32[2,96]{1,0:T(2,128)S(1)}, f32[2,96]{1,0:T(2,128)S(1)}, s32[2]{0:T(128)S(1)}, /*index=5*/f32[2,96,...) while((s32[]{:T(128)}, f32[64,128]{1,0:T(8,128)S(1)}, ...), condition=%wide.region_3.0_spmd.clone.clone, body=%wide.region_0.0_spmd.clone.clone.sunk | while | flops 5445426688 | bytes 89226920 | solution.py:64
  48.1 0.6 dynamic_slice.62
  48.7 0.6 compare_convert_fusion.2
  49.3 0.2 fusion.42
  49.5 0.1 copy.48
  49.6 0.1 copy.49
  49.7 1.8 %broadcast_multiply_fusion.4 = (f32[96,64,128]{2,1,0:T(8,128)S(1)}, f32[96,64,128]{2,1,0:T(8,128)S(1)}) fusion(f32[96,64]{1,0:T(8,128)S(1)} %copy.48, f32[96,128]{1,0:T(8,128)S(1)} %dynamic-slice_bitcast_fusion.4, f32[96,64]{1,0:T(8,128)S(1)} %copy.49), kind=kLoop, calls=%fused_computation.9.clone.1 | loop fusion | flops 1572864 | bytes 6389760 | tf_op jit(solution)/shard_map/while/body/eval_jaxpr/mul | solution.py:17
  51.5 2.2 %bitcast_dynamic-update-slice_fusion.4 = f32[192,8192]{1,0:T(8,128)S(1)} fusion(f32[12,8,64,128]{3,2,1,0:T(8,128)S(1)} %bitcast.112), kind=kLoop, calls=%fused_computation.6.clone.1 | loop fusion | bytes 6291456 | tf_op jit(solution)/shard_map/while
  53.7 2.2 %bitcast_dynamic-update-slice_fusion.5 = f32[192,8192]{1,0:T(8,128)S(1)} fusion(f32[192,8192]{1,0:T(8,128)S(1)} %bitcast_dynamic-update-slice_fusion.4, f32[12,8,64,128]{3,2,1,0:T(8,128)S(1)} %bitcast.111), kind=kLoop, calls=%fused_computation.5.clone.1 | loop fusion | bytes 6291456 | tf_op jit(solution)/shard_map/while/body/eval_jaxpr/concatenate | solution.py:54
  55.9 2.6 %copy-done = f32[192,8192]{1,0:T(8,128)} copy-done((f32[192,8192]{1,0:T(8,128)}, f32[192,8192]{1,0:T(8,128)S(1)}, u32[]{:S(2)}) %copy-start) | copy-done | bytes 6291480 | tf_op jit(solution)/shard_map/while
  58.5 6.4 %fusion.44 = f32[8192]{0:T(1024)S(1)} fusion(f32[192,8192]{1,0:T(8,128)S(1)} %bitcast_dynamic-update-slice_fusion.5, f32[96,96]{1,0:T(8,128)S(1)} %get-tuple-element.301, f32[96,96]{1,0:T(8,128)S(1)} %get-tuple-element.302, f32[96,96]{1,0:T(8,128)S(1)} %fusion.43), kind=kOutput, calls=%fused_computation.8.clone.1 | convolution fusion | flops 3627126784 | bytes 6434816 | tf_op jit(solution)/shard_map/while/body/eval_jaxpr/dot_general | solution.py:55
  64.9 3.2 %pad_maximum_fusion.3 = f32[192,64,128]{2,1,0:T(8,128)} fusion(f32[96,64,128]{2,1,0:T(8,128)S(1)} %get-tuple-element.300, f32[96,64,128]{2,1,0:T(8,128)S(1)} %get-tuple-element.299), kind=kLoop, calls=%fused_computation.4.clone.1 | loop fusion | flops 1572864 | bytes 12582912 | tf_op jit(solution)/shard_map/while/body/eval_jaxpr/concatenate | solution.py:54
  68.0 7.2 %reshape.257 = f32[2,96,8192]{2,1,0:T(8,128)} reshape(f32[192,64,128]{2,1,0:T(8,128)} %pad_maximum_fusion.3) | data formatting | bytes 12582912 | tf_op jit(solution)/shard_map/while/body/eval_jaxpr/reshape;while/body/eval_jaxpr/reshape | solution.py:57
  75.2 9.0 %fusion.45 = f32[8192]{0:T(1024)S(1)} fusion(f32[2,96,8192]{2,1,0:T(8,128)} %bitcast.110, f32[2,96,8192]{2,1,0:T(8,128)} %reshape.257, f32[3,1,96,96]{3,2,1,0:T(8,128)S(1)} %dynamic-slice_bitcast_fusion.5), kind=kOutput, calls=%fused_computation.7.clone.1 | convolution fusion | flops 1815076864 | bytes 12664832 | tf_op jit(solution)/shard_map/while/body/eval_jaxpr/mn,cnx->cmx/dot_general | solution.py:56
  84.3 0.6 dynamic_slice.62
  84.8 0.6 compare_convert_fusion.2
  85.4 0.2 fusion.42
  85.6 0.1 copy.48
  85.8 0.1 copy.49
  85.8 1.8 %broadcast_multiply_fusion.4 = (f32[96,64,128]{2,1,0:T(8,128)S(1)}, f32[96,64,128]{2,1,0:T(8,128)S(1)}) fusion(f32[96,64]{1,0:T(8,128)S(1)} %copy.48, f32[96,128]{1,0:T(8,128)S(1)} %dynamic-slice_bitcast_fusion.4, f32[96,64]{1,0:T(8,128)S(1)} %copy.49), kind=kLoop, calls=%fused_computation.9.clone.1 | loop fusion | flops 1572864 | bytes 6389760 | tf_op jit(solution)/shard_map/while/body/eval_jaxpr/mul | solution.py:17
  87.7 2.2 %bitcast_dynamic-update-slice_fusion.4 = f32[192,8192]{1,0:T(8,128)S(1)} fusion(f32[12,8,64,128]{3,2,1,0:T(8,128)S(1)} %bitcast.112), kind=kLoop, calls=%fused_computation.6.clone.1 | loop fusion | bytes 6291456 | tf_op jit(solution)/shard_map/while
  89.9 2.2 %bitcast_dynamic-update-slice_fusion.5 = f32[192,8192]{1,0:T(8,128)S(1)} fusion(f32[192,8192]{1,0:T(8,128)S(1)} %bitcast_dynamic-update-slice_fusion.4, f32[12,8,64,128]{3,2,1,0:T(8,128)S(1)} %bitcast.111), kind=kLoop, calls=%fused_computation.5.clone.1 | loop fusion | bytes 6291456 | tf_op jit(solution)/shard_map/while/body/eval_jaxpr/concatenate | solution.py:54
  92.1 2.6 %copy-done = f32[192,8192]{1,0:T(8,128)} copy-done((f32[192,8192]{1,0:T(8,128)}, f32[192,8192]{1,0:T(8,128)S(1)}, u32[]{:S(2)}) %copy-start) | copy-done | bytes 6291480 | tf_op jit(solution)/shard_map/while
  94.7 6.4 %fusion.44 = f32[8192]{0:T(1024)S(1)} fusion(f32[192,8192]{1,0:T(8,128)S(1)} %bitcast_dynamic-update-slice_fusion.5, f32[96,96]{1,0:T(8,128)S(1)} %get-tuple-element.301, f32[96,96]{1,0:T(8,128)S(1)} %get-tuple-element.302, f32[96,96]{1,0:T(8,128)S(1)} %fusion.43), kind=kOutput, calls=%fused_computation.8.clone.1 | convolution fusion | flops 3627126784 | bytes 6434816 | tf_op jit(solution)/shard_map/while/body/eval_jaxpr/dot_general | solution.py:55
  101.1 3.2 %pad_maximum_fusion.3 = f32[192,64,128]{2,1,0:T(8,128)} fusion(f32[96,64,128]{2,1,0:T(8,128)S(1)} %get-tuple-element.300, f32[96,64,128]{2,1,0:T(8,128)S(1)} %get-tuple-element.299), kind=kLoop, calls=%fused_computation.4.clone.1 | loop fusion | flops 1572864 | bytes 12582912 | tf_op jit(solution)/shard_map/while/body/eval_jaxpr/concatenate | solution.py:54
  104.2 7.2 %reshape.257 = f32[2,96,8192]{2,1,0:T(8,128)} reshape(f32[192,64,128]{2,1,0:T(8,128)} %pad_maximum_fusion.3) | data formatting | bytes 12582912 | tf_op jit(solution)/shard_map/while/body/eval_jaxpr/reshape;while/body/eval_jaxpr/reshape | solution.py:57
  111.4 9.0 %fusion.45 = f32[8192]{0:T(1024)S(1)} fusion(f32[2,96,8192]{2,1,0:T(8,128)} %bitcast.110, f32[2,96,8192]{2,1,0:T(8,128)} %reshape.257, f32[3,1,96,96]{3,2,1,0:T(8,128)S(1)} %dynamic-slice_bitcast_fusion.5), kind=kOutput, calls=%fused_computation.7.clone.1 | convolution fusion | flops 1815076864 | bytes 12664832 | tf_op jit(solution)/shard_map/while/body/eval_jaxpr/mn,cnx->cmx/dot_general | solution.py:56
  120.4 57.6 %all-reduce = f32[64,128]{1,0:T(8,128)S(1)} all-reduce(f32[64,128]{1,0:T(8,128)S(1)} %broadcast_multiply_fusion.2), channel_id=2, replica_groups=mesh['freq'=16,'grid'=2] {'freq'}, use_global_device_ids=true, to_apply=%region_4.0.clone | all-reduce | flops 8192 | bytes 65536
  178.1 0.6 constant_dynamic-slice_fusion.2
  (23 shorter events, 0.2 us)
Async XLA Ops:
  0.0 48.0 %copy-start.2 = (f32[2,96]{1,0:T(2,128)S(1)}, f32[2,96]{1,0:T(2,128)}, u32[]{:S(2)}) copy-start(f32[2,96]{1,0:T(2,128)} %param.12) | copy-start | bytes 2308
  0.0 48.0 %copy-start.3 = (f32[2,96]{1,0:T(2,128)S(1)}, f32[2,96]{1,0:T(2,128)}, u32[]{:S(2)}) copy-start(f32[2,96]{1,0:T(2,128)} %param.11) | copy-start | bytes 2308
  0.0 48.0 %copy-start.4 = (s32[2]{0:T(128)S(1)}, s32[2]{0:T(128)}, u32[]{:S(2)}) copy-start(s32[2]{0:T(128)} %param.13) | copy-start | bytes 28
  0.0 48.0 %copy-start.1 = (f32[2,96,128]{2,1,0:T(8,128)S(1)}, f32[2,96,128]{2,1,0:T(8,128)}, u32[]{:S(2)}) copy-start(f32[2,96,128]{2,1,0:T(8,128)} %param.10) | copy-start | bytes 294916
  22.6 7.6 %all-to-all-start = ((f32[2,96,128]{2,1,0:T(8,128)}), f32[2,96,128]{2,1,0:T(8,128)S(1)}, u32[]{:S(2)}, u32[]{:S(2)}) async-start(f32[2,96,128]{2,1,0:T(8,128)} %param.9), calls=%async_computation | async-start | bytes 196608 | tf_op jit(solution)/shard_map/all_to_all | solution.py:33
  30.3 10.9 %all-to-all-start.2 = ((f32[2,2,256,128]{3,2,0,1:T(8,128)}), f32[2,2,256,128]{3,2,0,1:T(8,128)S(1)}, u32[]{:S(2)}, u32[]{:S(2)}) async-start(f32[2,2,256,128]{3,2,0,1:T(8,128)} %bitcast.6), calls=%async_computation.2 | async-start | bytes 1048576 | tf_op jit(solution)/shard_map/all_to_all | solution.py:26
  55.9 2.6 %copy-start = (f32[192,8192]{1,0:T(8,128)}, f32[192,8192]{1,0:T(8,128)S(1)}, u32[]{:S(2)}) copy-start(f32[192,8192]{1,0:T(8,128)S(1)} %bitcast_dynamic-update-slice_fusion.5) | copy-start | bytes 18874372 | tf_op jit(solution)/shard_map/while
  92.0 2.6 %copy-start = (f32[192,8192]{1,0:T(8,128)}, f32[192,8192]{1,0:T(8,128)S(1)}, u32[]{:S(2)}) copy-start(f32[192,8192]{1,0:T(8,128)S(1)} %bitcast_dynamic-update-slice_fusion.5) | copy-start | bytes 18874372 | tf_op jit(solution)/shard_map/while
where the time goes:
time: 179 us
  blocking collectives  84.9 us (47%)
  local copies, waits for them, and re-layouts  34 us (19%)
  matrix products  31.9 us (18%)
  other arithmetic  11.6 us (6%)
  waiting for transfers between devices  8.41 us (5%)
  starting transfers between devices  6.83 us (4%)
    unnamed x1, blocking collectives  57.6 us
    all_to_all x1, blocking collectives, per_device(): lax.all_to_all(cross_spectra, 'freq', split_axis=1, concat_axis=2, tiled=...  21.5 us
    dot_general x2, matrix products, one_bin(): jnp.einsum('mn,cnx->cmx', block[2], coefs.reshape(2, modes, count * depth...  18 us
    reshape x2, local copies, waits for them, and re-layouts, one_bin(): coefs.reshape(2, modes, count * depth_here)  14.3 us
    dot_general x2, matrix products, one_bin(): image = jnp.dot(coupling, coefs, precision=HIGH)  12.7 us
    while x6, local copies, waits for them, and re-layouts  9.54 us
    concatenate x2, other arithmetic, one_bin(): jnp.concatenate([coef_real, coef_imag], 0)  6.34 us
    all_gather x1, blocking collectives, per_device(): spectra = lax.all_gather(stacked_local, 'grid', axis=1, tiled=True)  5.81 us
  transfers between devices with their start and end apart: 2, of which 2 were waited for; matrix products, arithmetic and copies ran while one was open for 1% of the time, Pallas kernels for 0%

commit v1 on v0

--- a/solution.py
+++ b/solution.py
@@ -5,6 +5,18 @@
 
 RANGES = 64
 HIGH = lax.Precision.HIGHEST
+
+
+def _attach_record(z_in, comm_axis, d_out, in_dim):
+    return jnp.concatenate(
+        lax.all_to_all(
+            jnp.stack(jnp.split(z_in, lax.axis_size(comm_axis), axis=d_out), axis=0),
+            comm_axis,
+            0,
+            0,
+        ),
+        axis=in_dim,
+    )
 
 
 def replica_terms(wave_row, atten_row, count, source_row, ranges):
@@ -24,11 +36,7 @@
     depth_here = source_modes.shape[2]
     total_bins = bins_here * lax.axis_size("freq")
     whole_spectra = lax.all_to_all(
-        lax.all_to_all(cross_spectra, "freq", split_axis=1, concat_axis=2, tiled=True),
-        "grid",
-        split_axis=1,
-        concat_axis=3,
-        tiled=True,
+        _attach_record(cross_spectra, "freq", 1, 2), "grid", split_axis=1, concat_axis=3, tiled=True
     )
     whole_modes = lax.all_to_all(sensor_modes, "grid", split_axis=0, concat_axis=2, tiled=True)
     product = jnp.einsum("cbij,bmj->cbim", whole_spectra, whole_modes, precision=HIGH)

time: 179 us -> 191 us (1.067)
  local copies, waits for them, and re-layouts: 34 us -> 45.1 us
    unnamed x11 -> x25, local copies, waits for them, and re-layouts: 3.04 us -> 13.4 us
where the time goes in v1:
time: 191 us; the launch traced here: 190 us
  blocking collectives  84.9 us (44%)
  local copies, waits for them, and re-layouts  45.1 us (24%)
  matrix products  31.9 us (17%)
  other arithmetic  11.6 us (6%)
  waiting for transfers between devices  8.38 us (4%)
  starting transfers between devices  6.83 us (4%)
    unnamed x1, blocking collectives  57.6 us
    all_to_all x1, blocking collectives, _attach_record(): lax.all_to_all(jnp.stack(jnp.split(z_in, lax.axis_size(comm_axis), axis=d...  21.5 us
    dot_general x2, matrix products, one_bin(): jnp.einsum('mn,cnx->cmx', block[2], coefs.reshape(2, modes, count * depth...  18 us
    reshape x2, local copies, waits for them, and re-layouts, one_bin(): coefs.reshape(2, modes, count * depth_here)  14.3 us
    unnamed x25, local copies, waits for them, and re-layouts  13.4 us
    dot_general x2, matrix products, one_bin(): image = jnp.dot(coupling, coefs, precision=HIGH)  12.7 us
    while x6, local copies, waits for them, and re-layouts  9.54 us
    concatenate x2, other arithmetic, one_bin(): jnp.concatenate([coef_real, coef_imag], 0)  6.34 us
  transfers between devices with their start and end apart: 2, of which 2 were waited for; matrix products, arithmetic and copies ran while one was open for 1% of the time, Pallas kernels for 0%

profile of v1, /device:TPU:0, one launch (start us, length us, event | category | flops | bytes accessed | tf_op | source)
XLA Modules:
  0.0 189.8 jit_solution(9682889852274238373)
XLA Ops:
  0.0 0.8 constant_dynamic-update-slice_fusion.15
  0.8 0.8 constant_dynamic-update-slice_fusion.14
  1.6 0.8 constant_dynamic-update-slice_fusion.13
  2.3 0.8 constant_dynamic-update-slice_fusion.12
  3.1 0.8 constant_dynamic-update-slice_fusion.11
  3.9 0.8 constant_dynamic-update-slice_fusion.10
  4.6 0.8 constant_dynamic-update-slice_fusion.9
  5.4 0.8 constant_dynamic-update-slice_fusion.8
  6.1 0.8 constant_dynamic-update-slice_fusion.7
  6.9 0.8 constant_dynamic-update-slice_fusion.6
  7.7 0.8 constant_dynamic-update-slice_fusion.5
  8.4 0.8 constant_dynamic-update-slice_fusion.4
  9.2 0.8 constant_dynamic-update-slice_fusion.3
  10.0 0.8 constant_dynamic-update-slice_fusion.2
  10.7 0.8 constant_dynamic-update-slice_fusion.1
  11.5 0.8 constant_dynamic-update-slice_fusion
  12.2 21.5 %all_to_all.35 = f32[16,2,2,16,128]{4,3,2,1,0:T(8,128)S(1)} all-to-all(f32[16,2,2,16,128]{4,3,2,1,0:T(8,128)S(1)} %constant_dynamic-update-slice_fusion), channel_id=1, replica_groups=mesh['freq'=16,'grid'=2] {'freq'}, dimensions={0} | all-to-all | bytes 1048576 | tf_op jit(solution)/shard_map/all_to_all | solution.py:12
  33.7 3.3 %all-to-all-start.2 = ((f32[2,96,128]{2,1,0:T(8,128)}), f32[2,96,128]{2,1,0:T(8,128)S(1)}, u32[]{:S(2)}, u32[]{:S(2)}) async-start(f32[2,96,128]{2,1,0:T(8,128)} %param.9), calls=%async_computation.2 | async-start | bytes 196608 | tf_op jit(solution)/shard_map/all_to_all | solution.py:41
  37.1 0.8 copy.29
  37.9 3.4 %all-to-all-done.2 = f32[2,96,128]{2,1,0:T(8,128)S(1)} async-done(((f32[2,96,128]{2,1,0:T(8,128)}), f32[2,96,128]{2,1,0:T(8,128)S(1)}, u32[]{:S(2)}, u32[]{:S(2)}) %all-to-all-start.2) | async-done | bytes 98336 | tf_op jit(solution)/shard_map/all_to_all | solution.py:41
  41.3 3.5 %all-to-all-start.1 = ((f32[2,2,256,128]{3,2,0,1:T(8,128)}), f32[2,2,256,128]{3,2,0,1:T(8,128)S(1)}, u32[]{:S(2)}, u32[]{:S(2)}) async-start(f32[2,2,256,128]{3,2,0,1:T(8,128)} %copy.29), calls=%async_computation.1 | async-start | bytes 1048576 | tf_op jit(solution)/shard_map/all_to_all | solution.py:38
  44.8 1.3 dynamic-slice
  47.3 5.0 %all-to-all-done.1 = f32[2,2,256,128]{3,2,0,1:T(8,128)S(1)} async-done(((f32[2,2,256,128]{3,2,0,1:T(8,128)}), f32[2,2,256,128]{3,2,0,1:T(8,128)S(1)}, u32[]{:S(2)}, u32[]{:S(2)}) %all-to-all-start.1) | async-done | bytes 524320 | tf_op jit(solution)/shard_map/all_to_all | solution.py:38
  52.2 0.6 convolution_bitcast_fusion.1
  53.3 5.8 %all_gather.3 = f32[3,2,96,96]{3,2,0,1:T(8,128)S(1)} all-gather(f32[3,1,96,96]{3,2,0,1:T(8,128)S(1)} %copy.33), channel_id=1, replica_groups=mesh['freq'=16,'grid'=2] {'grid'}, dimensions={1}, use_global_device_ids=true | all-gather | bytes 331776 | tf_op jit(solution)/shard_map/all_gather | solution.py:46
  59.2 72.4 %while.15 = (s32[]{:T(128)}, f32[64,128]{1,0:T(8,128)S(1)}, f32[2,96]{1,0:T(2,128)S(1)}, f32[2,96]{1,0:T(2,128)S(1)}, s32[2]{0:T(128)S(1)}, /*index=5*/f32[2,96,...) while((s32[]{:T(128)}, f32[64,128]{1,0:T(8,128)S(1)}, ...), condition=%wide.region_3.0_spmd.clone.clone, body=%wide.region_0.0_spmd.clone.clone.sunk | while | flops 5445426688 | bytes 89226920 | solution.py:72
  59.2 0.6 dynamic_slice.62
  59.8 0.6 compare_convert_fusion.2
  60.8 1.8 broadcast_multiply_fusion.4
  62.6 2.2 %bitcast_dynamic-update-slice_fusion.4 = f32[192,8192]{1,0:T(8,128)S(1)} fusion(f32[12,8,64,128]{3,2,1,0:T(8,128)S(1)} %bitcast.138), kind=kLoop, calls=%fused_computation.6.clone.1 | loop fusion | bytes 6291456 | tf_op jit(solution)/shard_map/while
  64.8 2.2 %bitcast_dynamic-update-slice_fusion.5 = f32[192,8192]{1,0:T(8,128)S(1)} fusion(f32[192,8192]{1,0:T(8,128)S(1)} %bitcast_dynamic-update-slice_fusion.4, f32[12,8,64,128]{3,2,1,0:T(8,128)S(1)} %bitcast.137), kind=kLoop, calls=%fused_computation.5.clone.1 | loop fusion | bytes 6291456 | tf_op jit(solution)/shard_map/while/body/eval_jaxpr/concatenate | solution.py:62
  67.0 2.6 %copy-done = f32[192,8192]{1,0:T(8,128)} copy-done((f32[192,8192]{1,0:T(8,128)}, f32[192,8192]{1,0:T(8,128)S(1)}, u32[]{:S(2)}) %copy-start) | copy-done | bytes 6291480 | tf_op jit(solution)/shard_map/while
  69.6 6.4 %fusion.44 = f32[8192]{0:T(1024)S(1)} fusion(f32[192,8192]{1,0:T(8,128)S(1)} %bitcast_dynamic-update-slice_fusion.5, f32[96,96]{1,0:T(8,128)S(1)} %get-tuple-element.308, f32[96,96]{1,0:T(8,128)S(1)} %get-tuple-element.309, f32[96,96]{1,0:T(8,128)S(1)} %fusion.43), kind=kOutput, calls=%fused_computation.8.clone.1 | convolution fusion | flops 3627126784 | bytes 6434816 | tf_op jit(solution)/shard_map/while/body/eval_jaxpr/dot_general | solution.py:63
  76.0 3.2 %pad_maximum_fusion.3 = f32[192,64,128]{2,1,0:T(8,128)} fusion(f32[96,64,128]{2,1,0:T(8,128)S(1)} %get-tuple-element.307, f32[96,64,128]{2,1,0:T(8,128)S(1)} %get-tuple-element.306), kind=kLoop, calls=%fused_computation.4.clone.1 | loop fusion | flops 1572864 | bytes 12582912 | tf_op jit(solution)/shard_map/while/body/eval_jaxpr/concatenate | solution.py:62
  79.2 7.2 %reshape.262 = f32[2,96,8192]{2,1,0:T(8,128)} reshape(f32[192,64,128]{2,1,0:T(8,128)} %pad_maximum_fusion.3) | data formatting | bytes 12582912 | tf_op jit(solution)/shard_map/while/body/eval_jaxpr/reshape;while/body/eval_jaxpr/reshape | solution.py:65
  86.3 9.0 %fusion.45 = f32[8192]{0:T(1024)S(1)} fusion(f32[2,96,8192]{2,1,0:T(8,128)} %bitcast.136, f32[2,96,8192]{2,1,0:T(8,128)} %reshape.262, f32[3,1,96,96]{3,2,1,0:T(8,128)S(1)} %dynamic-slice_bitcast_fusion.5), kind=kOutput, calls=%fused_computation.7.clone.1 | convolution fusion | flops 1815076864 | bytes 12664832 | tf_op jit(solution)/shard_map/while/body/eval_jaxpr/mn,cnx->cmx/dot_general | solution.py:64
  95.4 0.6 dynamic_slice.62
  96.0 0.6 compare_convert_fusion.2
  97.0 1.8 broadcast_multiply_fusion.4
  98.8 2.2 %bitcast_dynamic-update-slice_fusion.4 = f32[192,8192]{1,0:T(8,128)S(1)} fusion(f32[12,8,64,128]{3,2,1,0:T(8,128)S(1)} %bitcast.138), kind=kLoop, calls=%fused_computation.6.clone.1 | loop fusion | bytes 6291456 | tf_op jit(solution)/shard_map/while
  101.0 2.2 %bitcast_dynamic-update-slice_fusion.5 = f32[192,8192]{1,0:T(8,128)S(1)} fusion(f32[192,8192]{1,0:T(8,128)S(1)} %bitcast_dynamic-update-slice_fusion.4, f32[12,8,64,128]{3,2,1,0:T(8,128)S(1)} %bitcast.137), kind=kLoop, calls=%fused_computation.5.clone.1 | loop fusion | bytes 6291456 | tf_op jit(solution)/shard_map/while/body/eval_jaxpr/concatenate | solution.py:62
  103.2 2.6 %copy-done = f32[192,8192]{1,0:T(8,128)} copy-done((f32[192,8192]{1,0:T(8,128)}, f32[192,8192]{1,0:T(8,128)S(1)}, u32[]{:S(2)}) %copy-start) | copy-done | bytes 6291480 | tf_op jit(solution)/shard_map/while
  105.8 6.4 %fusion.44 = f32[8192]{0:T(1024)S(1)} fusion(f32[192,8192]{1,0:T(8,128)S(1)} %bitcast_dynamic-update-slice_fusion.5, f32[96,96]{1,0:T(8,128)S(1)} %get-tuple-element.308, f32[96,96]{1,0:T(8,128)S(1)} %get-tuple-element.309, f32[96,96]{1,0:T(8,128)S(1)} %fusion.43), kind=kOutput, calls=%fused_computation.8.clone.1 | convolution fusion | flops 3627126784 | bytes 6434816 | tf_op jit(solution)/shard_map/while/body/eval_jaxpr/dot_general | solution.py:63
  112.2 3.2 %pad_maximum_fusion.3 = f32[192,64,128]{2,1,0:T(8,128)} fusion(f32[96,64,128]{2,1,0:T(8,128)S(1)} %get-tuple-element.307, f32[96,64,128]{2,1,0:T(8,128)S(1)} %get-tuple-element.306), kind=kLoop, calls=%fused_computation.4.clone.1 | loop fusion | flops 1572864 | bytes 12582912 | tf_op jit(solution)/shard_map/while/body/eval_jaxpr/concatenate | solution.py:62
  115.3 7.2 %reshape.262 = f32[2,96,8192]{2,1,0:T(8,128)} reshape(f32[192,64,128]{2,1,0:T(8,128)} %pad_maximum_fusion.3) | data formatting | bytes 12582912 | tf_op jit(solution)/shard_map/while/body/eval_jaxpr/reshape;while/body/eval_jaxpr/reshape | solution.py:65
  122.5 9.0 %fusion.45 = f32[8192]{0:T(1024)S(1)} fusion(f32[2,96,8192]{2,1,0:T(8,128)} %bitcast.136, f32[2,96,8192]{2,1,0:T(8,128)} %reshape.262, f32[3,1,96,96]{3,2,1,0:T(8,128)S(1)} %dynamic-slice_bitcast_fusion.5), kind=kOutput, calls=%fused_computation.7.clone.1 | convolution fusion | flops 1815076864 | bytes 12664832 | tf_op jit(solution)/shard_map/while/body/eval_jaxpr/mn,cnx->cmx/dot_general | solution.py:64
  131.6 57.6 %all-reduce = f32[64,128]{1,0:T(8,128)S(1)} all-reduce(f32[64,128]{1,0:T(8,128)S(1)} %broadcast_multiply_fusion.2), channel_id=2, replica_groups=mesh['freq'=16,'grid'=2] {'freq'}, use_global_device_ids=true, to_apply=%region_4.0.clone | all-reduce | flops 8192 | bytes 65536
  189.2 0.6 constant_dynamic-slice_fusion.2
  (39 shorter events, 1.8 us)
Async XLA Ops:
  0.0 59.2 %copy-start.2 = (f32[2,96]{1,0:T(2,128)S(1)}, f32[2,96]{1,0:T(2,128)}, u32[]{:S(2)}) copy-start(f32[2,96]{1,0:T(2,128)} %param.12) | copy-start | bytes 2308
  0.0 59.2 %copy-start.3 = (f32[2,96]{1,0:T(2,128)S(1)}, f32[2,96]{1,0:T(2,128)}, u32[]{:S(2)}) copy-start(f32[2,96]{1,0:T(2,128)} %param.11) | copy-start | bytes 2308
  0.0 59.2 %copy-start.4 = (s32[2]{0:T(128)S(1)}, s32[2]{0:T(128)}, u32[]{:S(2)}) copy-start(s32[2]{0:T(128)} %param.13) | copy-start | bytes 28
  0.0 59.2 %copy-start.1 = (f32[2,96,128]{2,1,0:T(8,128)S(1)}, f32[2,96,128]{2,1,0:T(8,128)}, u32[]{:S(2)}) copy-start(f32[2,96,128]{2,1,0:T(8,128)} %param.10) | copy-start | bytes 294916
  33.7 7.6 %all-to-all-start.2 = ((f32[2,96,128]{2,1,0:T(8,128)}), f32[2,96,128]{2,1,0:T(8,128)S(1)}, u32[]{:S(2)}, u32[]{:S(2)}) async-start(f32[2,96,128]{2,1,0:T(8,128)} %param.9), calls=%async_computation.2 | async-start | bytes 196608 | tf_op jit(solution)/shard_map/all_to_all | solution.py:41
  41.3 10.9 %all-to-all-start.1 = ((f32[2,2,256,128]{3,2,0,1:T(8,128)}), f32[2,2,256,128]{3,2,0,1:T(8,128)S(1)}, u32[]{:S(2)}, u32[]{:S(2)}) async-start(f32[2,2,256,128]{3,2,0,1:T(8,128)} %copy.29), calls=%async_computation.1 | async-start | bytes 1048576 | tf_op jit(solution)/shard_map/all_to_all | solution.py:38
  67.0 2.6 %copy-start = (f32[192,8192]{1,0:T(8,128)}, f32[192,8192]{1,0:T(8,128)S(1)}, u32[]{:S(2)}) copy-start(f32[192,8192]{1,0:T(8,128)S(1)} %bitcast_dynamic-update-slice_fusion.5) | copy-start | bytes 18874372 | tf_op jit(solution)/shard_map/while
  103.2 2.6 %copy-start = (f32[192,8192]{1,0:T(8,128)}, f32[192,8192]{1,0:T(8,128)S(1)}, u32[]{:S(2)}) copy-start(f32[192,8192]{1,0:T(8,128)S(1)} %bitcast_dynamic-update-slice_fusion.5) | copy-start | bytes 18874372 | tf_op jit(solution)/shard_map/while
